TPU v7x, 32 devices: a whole 2x2x4 slice. The times are simulated.
32 devices in a mesh: row: 8 (over y, x, core), col: 4 (over z).
Axes of the slice: x: 2, y: 2, z: 4, core: 2. Of those that a mesh axis runs over, the one named last changes fastest.
Arguments:
- points: bfloat16 [4096, 128], P(('row', 'col')), may hold values from -6 to 6
- abar: bfloat16 [4096, 8, 4, 128], P('row', None, 'col'), may hold values from -6 to 6
- inv_scale: float32 [128], replicated, may hold values from 0.05 to 0.2
Outputs:
- point_grad: float32 [4096, 128], P(('row', 'col'))
All inputs are finite; a program needn't handle non-finite values.
Results may differ from a plain program's by a relative error of at most 0.0052.
Values may be sent and summed in bfloat16 or wider, within the bound.
A program may use at most 64 MiB of HBM per device.

v0:
```python
import functools

import jax
import jax.numpy as jnp
from jax import lax
from jax.experimental import pallas as pl
from jax.experimental.pallas import tpu as pltpu
from jax.sharding import PartitionSpec as P

MESH = pl.DeviceIdType.MESH
F32, BF16 = jnp.float32, jnp.bfloat16


def augment(block, left):
    wide = block.astype(F32)
    half = -0.5 * jnp.sum(wide * wide, axis=1, keepdims=True)
    high = half.astype(BF16).astype(F32)
    mid = (half - high).astype(BF16).astype(F32)
    low = half - high - mid
    lane = lax.broadcasted_iota(jnp.int32, wide.shape, 1)
    shift = 0 if left else 3
    parts = jnp.where(lane == shift, high, 0.0)
    parts = jnp.where(lane == shift + 1, mid, parts)
    parts = jnp.where(lane == shift + 2, low, parts)
    ones = (lane >= 3 - shift) & (lane < 6 - shift)
    parts = jnp.where(ones, 1.0, parts)
    return jnp.concatenate([block, parts.astype(BF16)], axis=1)


def partner(index, k, count):
    if count & (count - 1):
        return lax.rem(index + k, count)
    out, bit = 0, 1
    while bit < count:
        digit = (index // bit) % 2
        out = out + bit * ((1 - digit) if k & bit else digit)
        bit *= 2
    return out


def returns_to(index, k, count):
    if count & (count - 1):
        return lax.rem(index + count - k, count)
    return partner(index, k, count)


def kernel(
    n_row, n_col, pts_hbm, inv_hbm, ab_hbm, out_ref,
    pts_v, inv_v, ab_v, af, scaled_v, rows_v, cols_v, left, right, row_one, col_one, acc, sec,
    first_out, second_out, first_in, second_in,
    load_sem, rows_send, rows_recv, cols_send, cols_recv,
    first_send, first_recv, second_send, second_recv,
):
    r, c = lax.axis_index("row"), lax.axis_index("col")
    size, feat = pts_v.shape
    rows = n_col * size
    row_to = [partner(r, k, n_row) for k in range(n_row)]
    col_to = [partner(c, k, n_col) for k in range(n_col)]
    row_from = [returns_to(r, k, n_row) for k in range(n_row)]
    col_from = [returns_to(c, k, n_col) for k in range(n_col)]

    barrier = pltpu.get_barrier_semaphore()
    for k in reversed(range(1, n_col)):
        pl.semaphore_signal(barrier, inc=1, device_id=(r, col_to[k]), device_id_type=MESH)
    for k in reversed(range(1, n_row)):
        pl.semaphore_signal(barrier, inc=1, device_id=(row_to[k], c), device_id_type=MESH)
    loads = [
        pltpu.make_async_copy(src, dst, load_sem.at[k])
        for k, (src, dst) in enumerate([(pts_hbm, pts_v), (inv_hbm, inv_v), (ab_hbm, ab_v)])
    ]
    for load in loads:
        load.start()
    loads[0].wait()
    loads[1].wait()
    scaled = (pts_v[...].astype(F32) * inv_v[...]).astype(BF16)
    scaled_v[...] = scaled

    ones = jnp.ones((size, feat), BF16)

    def place_row(k, block):
        left[k * size : (k + 1) * size] = augment(block, True)
        row_one[k * size : (k + 1) * size] = jnp.concatenate([block, ones], axis=1)

    def place_col(k, block):
        right[k * size : (k + 1) * size] = augment(block, False)
        col_one[k * size : (k + 1) * size] = jnp.concatenate([block, ones], axis=1)

    place_row(0, scaled)
    place_col(0, scaled)
    loads[2].wait()
    step = min(rows, 128)

    def widen(i, carry):
        at = pl.multiple_of(i * step, step)
        part = ab_v[pl.ds(at, step)].astype(F32)
        af[pl.ds(pl.multiple_of(at * n_row, step), step * n_row)] = part.reshape(step * n_row, size)
        return carry

    lax.fori_loop(0, rows // step, widen, 0)
    acc[...] = jnp.zeros_like(acc)
    sec[...] = jnp.zeros_like(sec)
    pl.semaphore_wait(barrier, n_col + n_row - 2)

    def send(src, dst, send_sem, recv_sem, device):
        return pltpu.make_async_remote_copy(
            src_ref=src, dst_ref=dst, send_sem=send_sem, recv_sem=recv_sem,
            device_id=device, device_id_type=MESH,
        )

    def row_copy(k):
        return send(scaled_v, rows_v.at[k], rows_send.at[k], rows_recv.at[k], (r, col_to[k]))

    def col_copy(k):
        return send(scaled_v, cols_v.at[k], cols_send.at[k], cols_recv.at[k], (row_to[k], c))

    def first_copy(k):
        return send(
            first_out.at[k], first_in.at[k], first_send.at[k], first_recv.at[k], (r, col_from[k])
        )

    def second_copy(k):
        return send(
            second_out.at[k], second_in.at[k], second_send.at[k], second_recv.at[k], (row_from[k], c)
        )

    for k in reversed(range(1, n_col)):
        row_copy(k).start()
    for k in reversed(range(1, n_row)):
        col_copy(k).start()

    def compute(r0, r1, c0, c1):
        if r0 >= r1:
            return
        for k in range(c0, c1, 2):
            some = range(k, min(k + 2, c1))
            lo, hi = k * size, (some[-1] + 1) * size
            exponent = lax.dot_general(
                left[r0 * size : r1 * size], right[lo:hi], (((1,), (1,)), ((), ())),
                preferred_element_type=F32,
            )
            factors = jnp.concatenate([
                jnp.concatenate([
                    af[pl.ds(col_from[i] * (size * n_row) + row_from[j], size, stride=n_row), :]
                    for i in range(r0, r1)
                ], axis=0)
                for j in some
            ], axis=1)
            weighted = (factors * jnp.exp(exponent)).astype(BF16)
            acc[r0 * size : r1 * size] += jnp.dot(
                weighted, col_one[lo:hi], preferred_element_type=F32
            )
            sec[lo:hi] += lax.dot_general(
                weighted, row_one[r0 * size : r1 * size], (((0,), (0,)), ((), ())),
                preferred_element_type=F32,
            )

    def finish(total, one, k):
        both = total[k * size : (k + 1) * size]
        block = one[k * size : (k + 1) * size, :feat].astype(F32)
        return both[:, feat:] * block - both[:, :feat]

    near_r, near_c = max(1, n_row), max(1, n_col)
    for k in range(1, near_c):
        row_copy(k).wait_recv()
    for k in range(1, near_r):
        col_copy(k).wait_recv()
    for k in range(1, near_c):
        place_row(k, rows_v[k])
    for k in range(1, near_r):
        place_col(k, cols_v[k])
    compute(0, near_c, 0, near_r)
    for k in range(near_c, n_col):
        row_copy(k).wait_recv()
    for k in range(near_r, n_row):
        col_copy(k).wait_recv()
    for k in range(near_c, n_col):
        place_row(k, rows_v[k])
    for k in range(near_r, n_row):
        place_col(k, cols_v[k])
    compute(0, n_col, near_r, n_row)
    compute(near_c, n_col, 0, near_r)

    pending = None
    for k in reversed(range(1, n_col)):
        first_out[k] = finish(acc, row_one, k).astype(BF16)
        if pending is not None:
            pending.start()
        pending = first_copy(k)
    for k in reversed(range(1, n_row)):
        second_out[k] = finish(sec, col_one, k).astype(BF16)
        if pending is not None:
            pending.start()
        pending = second_copy(k)
    total = finish(acc, row_one, 0) + finish(sec, col_one, 0)
    out_ref[...] = total
    if pending is not None:
        pending.start()
    for k in range(1, n_row):
        second_copy(k).wait_recv()
    for k in range(1, n_col):
        first_copy(k).wait_recv()
    for k in range(1, n_row):
        total = total + second_in[k].astype(F32)
    for k in range(1, n_col):
        total = total + first_in[k].astype(F32)
    out_ref[...] = total
    for k in range(1, n_col):
        row_copy(k).wait_send()
        first_copy(k).wait_send()
    for k in range(1, n_row):
        col_copy(k).wait_send()
        second_copy(k).wait_send()


def per_device(n_row, n_col, points, abar, inv_scale):
    size, feat = points.shape
    rows = abar.shape[0]
    dma = pltpu.SemaphoreType.DMA
    any_space = pl.BlockSpec(memory_space=pl.ANY)
    total = pl.pallas_call(
        functools.partial(kernel, n_row, n_col),
        out_shape=jax.ShapeDtypeStruct((size, feat), F32),
        in_specs=[any_space] * 3,
        out_specs=pl.BlockSpec(memory_space=pltpu.VMEM),
        scratch_shapes=[
            pltpu.VMEM((size, feat), BF16),
            pltpu.VMEM((1, feat), F32),
            pltpu.VMEM((rows, n_row, size), BF16),
            pltpu.VMEM((rows * n_row, size), F32),
            pltpu.VMEM((size, feat), BF16),
            pltpu.VMEM((n_col, size, feat), BF16),
            pltpu.VMEM((n_row, size, feat), BF16),
            pltpu.VMEM((rows, 2 * feat), BF16),
            pltpu.VMEM((n_row * size, 2 * feat), BF16),
            pltpu.VMEM((rows, 2 * feat), BF16),
            pltpu.VMEM((n_row * size, 2 * feat), BF16),
            pltpu.VMEM((rows, 2 * feat), F32),
            pltpu.VMEM((n_row * size, 2 * feat), F32),
            pltpu.VMEM((n_col, size, feat), BF16),
            pltpu.VMEM((n_row, size, feat), BF16),
            pltpu.VMEM((n_col, size, feat), BF16),
            pltpu.VMEM((n_row, size, feat), BF16),
            dma((3,)),
            dma((n_col,)), dma((n_col,)), dma((n_row,)), dma((n_row,)),
            dma((n_col,)), dma((n_col,)), dma((n_row,)), dma((n_row,)),
        ],
        compiler_params=pltpu.CompilerParams(collective_id=0, has_side_effects=True),
    )(points, inv_scale.reshape(1, feat), abar.reshape(rows, n_row, size))
    return -total * inv_scale[None, :]


def solution(mesh):
    placed = (P(("row", "col"), None), P("row", None, "col", None), P())
    body = functools.partial(per_device, mesh.shape["row"], mesh.shape["col"])
    return jax.shard_map(
        body, mesh=mesh, in_specs=placed, out_specs=P(("row", "col"), None), check_vma=False
    )
```

profile of v0, /device:TPU:0, one launch (start us, length us, event | category | flops | bytes accessed | tf_op | source)
XLA Modules:
  0.0 19.0 jit_solution(7799467820054185882)
XLA Ops:
  0.0 0.0 copy-start
  0.0 17.5 %shard_map.37 = f32[128,128]{1,0:T(8,128)} custom-call(bf16[128,128]{1,0:T(8,128)(2,1)} %pts_hbm.1, f32[1,128]{1,0:T(1,128)} %bitcast.3, bf16[512,8,128]{2,1,0:T(8,128)(2,1)} %bitcast.2), custom_call_target="tpu_custom_call" | custom-call | tf_op jit(solution)/shard_map/pallas_call | solution.py:220
  17.5 0.0 copy-done
  17.5 1.5 %negate_multiply_fusion = f32[128,128]{1,0:T(8,128)} fusion(f32[128,128]{1,0:T(8,128)} %shard_map.37, f32[128]{0:T(128)S(1)} %copy-done), kind=kLoop, calls=%fused_computation | loop fusion | flops 32768 | bytes 131584 | tf_op jit(solution)/shard_map/mul | solution.py:249
Async XLA Ops:
  0.0 17.5 %copy-start = (f32[128]{0:T(128)S(1)}, f32[128]{0:T(128)}, u32[]{:S(2)}) copy-start(f32[128]{0:T(128)} %param.5) | copy-start | bytes 1540
where the time goes:
time: 19.1 us; the launch traced here: 19 us
  Pallas kernels  17.5 us (92%)
  other arithmetic  1.48 us (8%)
    pallas_call x1, Pallas kernels, per_device(): pl.pallas_call(functools.partial(kernel, n_row, n_col), out_shape=jax.Sha...  17.5 us
    mul x1, other arithmetic, per_device(): return -total * inv_scale[None, :]  1.48 us

commit v1 on v0

--- a/solution.py
+++ b/solution.py
@@ -75,6 +75,35 @@
     scaled = (pts_v[...].astype(F32) * inv_v[...]).astype(BF16)
     scaled_v[...] = scaled
 
+    pl.semaphore_wait(barrier, n_col + n_row - 2)
+
+    def send(src, dst, send_sem, recv_sem, device):
+        return pltpu.make_async_remote_copy(
+            src_ref=src, dst_ref=dst, send_sem=send_sem, recv_sem=recv_sem,
+            device_id=device, device_id_type=MESH,
+        )
+
+    def row_copy(k):
+        return send(scaled_v, rows_v.at[k], rows_send.at[k], rows_recv.at[k], (r, col_to[k]))
+
+    def col_copy(k):
+        return send(scaled_v, cols_v.at[k], cols_send.at[k], cols_recv.at[k], (row_to[k], c))
+
+    def first_copy(k):
+        return send(
+            first_out.at[k], first_in.at[k], first_send.at[k], first_recv.at[k], (r, col_from[k])
+        )
+
+    def second_copy(k):
+        return send(
+            second_out.at[k], second_in.at[k], second_send.at[k], second_recv.at[k], (row_from[k], c)
+        )
+
+    for k in reversed(range(1, n_col)):
+        row_copy(k).start()
+    for k in reversed(range(1, n_row)):
+        col_copy(k).start()
+
     ones = jnp.ones((size, feat), BF16)
 
     def place_row(k, block):
@@ -99,35 +128,6 @@
     lax.fori_loop(0, rows // step, widen, 0)
     acc[...] = jnp.zeros_like(acc)
     sec[...] = jnp.zeros_like(sec)
-    pl.semaphore_wait(barrier, n_col + n_row - 2)
-
-    def send(src, dst, send_sem, recv_sem, device):
-        return pltpu.make_async_remote_copy(
-            src_ref=src, dst_ref=dst, send_sem=send_sem, recv_sem=recv_sem,
-            device_id=device, device_id_type=MESH,
-        )
-
-    def row_copy(k):
-        return send(scaled_v, rows_v.at[k], rows_send.at[k], rows_recv.at[k], (r, col_to[k]))
-
-    def col_copy(k):
-        return send(scaled_v, cols_v.at[k], cols_send.at[k], cols_recv.at[k], (row_to[k], c))
-
-    def first_copy(k):
-        return send(
-            first_out.at[k], first_in.at[k], first_send.at[k], first_recv.at[k], (r, col_from[k])
-        )
-
-    def second_copy(k):
-        return send(
-            second_out.at[k], second_in.at[k], second_send.at[k], second_recv.at[k], (row_from[k], c)
-        )
-
-    for k in reversed(range(1, n_col)):
-        row_copy(k).start()
-    for k in reversed(range(1, n_row)):
-        col_copy(k).start()
-
     def compute(r0, r1, c0, c1):
         if r0 >= r1:
             return
@@ -203,7 +203,7 @@
         total = total + second_in[k].astype(F32)
     for k in range(1, n_col):
         total = total + first_in[k].astype(F32)
-    out_ref[...] = total
+    out_ref[...] = total * -inv_v[...]
     for k in range(1, n_col):
         row_copy(k).wait_send()
         first_copy(k).wait_send()
@@ -219,7 +219,7 @@
     any_space = pl.BlockSpec(memory_space=pl.ANY)
     total = pl.pallas_call(
         functools.partial(kernel, n_row, n_col),
-        out_shape=jax.ShapeDtypeStruct((size, feat), F32),
+        out_shape=pltpu.VMEM((size, feat), F32),
         in_specs=[any_space] * 3,
         out_specs=pl.BlockSpec(memory_space=pltpu.VMEM),
         scratch_shapes=[
@@ -246,7 +246,7 @@
         ],
         compiler_params=pltpu.CompilerParams(collective_id=0, has_side_effects=True),
     )(points, inv_scale.reshape(1, feat), abar.reshape(rows, n_row, size))
-    return -total * inv_scale[None, :]
+    return total
 
 
 def solution(mesh):

time: 19.1 us -> 17.7 us (0.927)
  other arithmetic: 1.48 us -> 0 us
  local copies, waits for them, and re-layouts: 0.01 us -> 0.63 us
  Pallas kernels: 17.5 us -> 16.9 us
    mul x1 -> x0, other arithmetic: 1.48 us -> none  [per_device(): return -total * inv_scale[None, :]]
    unnamed x2 -> x1, local copies, waits for them, and re-layouts: 0.01 us -> 0.63 us
    pallas_call x1, Pallas kernels: 17.5 us -> 16.9 us  [per_device(): pl.pallas_call(functools.partial(kernel, n_row, n_col), out_shape=pltpu.V...]
where the time goes in v1:
time: 17.7 us; the launch traced here: 17.6 us
  Pallas kernels  16.9 us (95%)
  local copies, waits for them, and re-layouts  0.63 us (4%)
    pallas_call x1, Pallas kernels, per_device(): pl.pallas_call(functools.partial(kernel, n_row, n_col), out_shape=pltpu.V...  16.9 us
    unnamed x1, local copies, waits for them, and re-layouts  0.63 us

profile of v1, /device:TPU:0, one launch (start us, length us, event | category | flops | bytes accessed | tf_op | source)
XLA Modules:
  0.0 17.6 jit_solution(16451310704399450972)
XLA Ops:
  0.0 16.9 %shard_map.37 = f32[128,128]{1,0:T(8,128)S(1)} custom-call(bf16[128,128]{1,0:T(8,128)(2,1)} %pts_hbm.1, f32[1,128]{1,0:T(1,128)} %bitcast.3, bf16[512,8,128]{2,1,0:T(8,128)(2,1)} %bitcast.2), custom_call_target="tpu_custom_call" | custom-call | tf_op jit(solution)/shard_map/pallas_call | solution.py:220
  16.9 0.6 %copy.5 = f32[128,128]{1,0:T(8,128)} copy(f32[128,128]{1,0:T(8,128)S(1)} %shard_map.37) | data formatting | bytes 131072

commit v2 on v1

v2 whole, which is shorter than its diff:
```python
import functools

import jax
import jax.numpy as jnp
from jax import lax
from jax.experimental import pallas as pl
from jax.experimental.pallas import tpu as pltpu
from jax.sharding import PartitionSpec as P

MESH = pl.DeviceIdType.MESH
F32, BF16 = jnp.float32, jnp.bfloat16


def partner(index, k, count):
    if count & (count - 1):
        return lax.rem(index + k, count)
    out, bit = 0, 1
    while bit < count:
        one, two = (index // bit) % 2, (k // bit) % 2
        out = out + bit * (one + two - 2 * one * two)
        bit *= 2
    return out


def returns_to(index, k, count):
    if count & (count - 1):
        return lax.rem(index + count - k, count)
    return partner(index, k, count)


def half_square(block):
    wide = block.astype(F32)
    return -0.5 * jnp.sum(wide * wide, axis=1, keepdims=True)


def marks(size, feat, first):
    lane = lax.broadcasted_iota(jnp.int32, (size, feat), 1)
    return jnp.where((lane >= first) & (lane < first + 3), 1.0, 0.0).astype(BF16)


def augment(block, left):
    half = half_square(block)
    high = half.astype(BF16).astype(F32)
    mid = (half - high).astype(BF16).astype(F32)
    low = half - high - mid
    lane = lax.broadcasted_iota(jnp.int32, block.shape, 1)
    shift = 0 if left else 3
    parts = jnp.where(lane == shift, high, 0.0)
    parts = jnp.where(lane == shift + 1, mid, parts)
    parts = jnp.where(lane == shift + 2, low, parts)
    ones = (lane >= 3 - shift) & (lane < 6 - shift)
    return jnp.where(ones, 1.0, parts).astype(BF16)


def kernel(
    n_row, n_col, pts_hbm, inv_hbm, ab_hbm, out_ref,
    pts_v, inv_v, ab_v, af, rows_v, cols_v, left_aug, right_aug, row_t, col_t,
    weighted, acc, sec,
    first_out, second_out, first_in, second_in,
    load_sem, rows_send, rows_recv, cols_send, cols_recv,
    first_send, first_recv, second_send, second_recv,
):
    r, c = lax.axis_index("row"), lax.axis_index("col")
    size, feat = pts_v.shape
    rows = n_col * size
    row_to = [partner(r, k, n_row) for k in range(n_row)]
    col_to = [partner(c, k, n_col) for k in range(n_col)]
    row_from = [returns_to(r, k, n_row) for k in range(n_row)]
    col_from = [returns_to(c, k, n_col) for k in range(n_col)]

    barrier = pltpu.get_barrier_semaphore()
    for k in reversed(range(1, n_col)):
        pl.semaphore_signal(barrier, inc=1, device_id=(r, col_to[k]), device_id_type=MESH)
    for k in reversed(range(1, n_row)):
        pl.semaphore_signal(barrier, inc=1, device_id=(row_to[k], c), device_id_type=MESH)
    loads = [
        pltpu.make_async_copy(src, dst, load_sem.at[k])
        for k, (src, dst) in enumerate([(pts_hbm, pts_v), (inv_hbm, inv_v), (ab_hbm, ab_v)])
    ]
    for load in loads:
        load.start()
    loads[0].wait()
    loads[1].wait()
    own = (pts_v[...].astype(F32) * inv_v[...]).astype(BF16)
    rows_v[0] = own
    cols_v[0] = own
    pl.semaphore_wait(barrier, n_col + n_row - 2)

    def send(src, dst, send_sem, recv_sem, device):
        return pltpu.make_async_remote_copy(
            src_ref=src, dst_ref=dst, send_sem=send_sem, recv_sem=recv_sem,
            device_id=device, device_id_type=MESH,
        )

    def row_copy(k):
        return send(rows_v.at[0], rows_v.at[k], rows_send.at[k], rows_recv.at[k], (r, partner(c, k, n_col)))

    def col_copy(k):
        return send(rows_v.at[0], cols_v.at[k], cols_send.at[k], cols_recv.at[k], (row_to[k], c))

    def first_copy(k):
        return send(
            first_out.at[k], first_in.at[k], first_send.at[k], first_recv.at[k],
            (r, returns_to(c, k, n_col)),
        )

    def second_copy(k):
        return send(
            second_out.at[k], second_in.at[k], second_send.at[k], second_recv.at[k], (row_from[k], c)
        )

    def farthest_first(copy_of):
        if n_col & (n_col - 1):
            for k in range(1, n_col):
                copy_of(k).start()
            return
        for d in reversed(range(1, n_col)):
            @pl.when(c >= d)
            def _():
                copy_of(partner(c, c - d, n_col)).start()

            @pl.when(c + d < n_col)
            def _():
                copy_of(partner(c, c + d, n_col)).start()

    for k in reversed(range(1, n_row)):
        col_copy(k).start()
    farthest_first(row_copy)

    left_aug[0] = augment(own, True)
    right_aug[0] = augment(own, False)
    own_t = own.T
    col_t[0] = own_t
    loads[2].wait()
    step = min(rows, 128)

    def widen(i, carry):
        at = pl.multiple_of(i * step, step)
        part = ab_v[pl.ds(at, step)].astype(F32)
        af[pl.ds(pl.multiple_of(at * n_row, step), step * n_row)] = part.reshape(step * n_row, size)
        return carry

    lax.fori_loop(0, rows // step, widen, 0)

    early = n_col
    late = list(range(early, n_col))
    wide = n_row * size
    extra = row_t.shape[0] - feat
    groups = [(k, min(k + 2, n_row)) for k in range(0, n_row, 2)]
    cut = (len(groups) + 1) // 2
    chunks = [groups[:1] + groups[cut + 1 :], groups[1 : cut + 1]]

    def joined(block, other):
        return jnp.concatenate([block, other], axis=1)

    def stack(parts):
        return jnp.concatenate(parts, axis=0) if len(parts) > 1 else parts[0]

    def weigh(some_rows, left, half, groups):
        top, low = some_rows[0] * size, (some_rows[-1] + 1) * size
        for begin, end in groups:
            right = stack([joined(cols_v[j], right_aug[j]) for j in range(begin, end)])
            exponent = lax.dot_general(
                left, right, (((1,), (1,)), ((), ())), preferred_element_type=F32
            )
            if half is not None:
                exponent = exponent + half
            factors = jnp.concatenate([
                stack([
                    af[pl.ds(col_from[i] * (size * n_row) + row_from[j], size, stride=n_row), :]
                    for i in some_rows
                ])
                for j in range(begin, end)
            ], axis=1)
            weighted[top:low, begin * size : end * size] = (
                factors * jnp.exp(exponent)
            ).astype(BF16)
        spans = [(begin * size, end * size) for begin, end in groups]
        block = jnp.concatenate([weighted[top:low, begin:end] for begin, end in spans], axis=1)
        every = stack([
            joined(cols_v[j], jnp.ones((size, feat), BF16))
            for begin, end in groups for j in range(begin, end)
        ])
        by_row = jnp.dot(block, every, preferred_element_type=F32)
        by_col = jnp.dot(row_t[:, top:low], block, preferred_element_type=F32)
        return by_row, by_col

    def finish(both, block):
        return both[:, feat:] * block.astype(F32) - both[:, :feat]

    row_t[feat:] = jnp.ones((extra, rows), BF16)
    row_t[:feat, :size] = own_t
    for k in range(1, early):
        row_copy(k).wait_recv()
    for k in range(1, early):
        left_aug[k] = augment(rows_v[k], True)
        row_t[:feat, k * size : (k + 1) * size] = rows_v[k].T
    pending = [None]

    def queue(copy):
        if pending[0] is not None:
            pending[0].start()
        pending[0] = copy

    def turned(k):
        both = sec[:, k * size : (k + 1) * size]
        return both[feat : feat + 1] * col_t[k].astype(F32) - both[:feat]

    for at, chunk in enumerate(chunks):
        members = [k for begin, end in chunk for k in range(begin, end)]
        for k in members:
            if k:
                col_copy(k).wait_recv()
        for k in members:
            if k:
                right_aug[k] = augment(cols_v[k], False)
                col_t[k] = cols_v[k].T
        by_row, by_col = weigh(
            list(range(early)),
            stack([joined(rows_v[i], left_aug[i]) for i in range(early)]), None, chunk,
        )
        if at == 0:
            acc[...] = by_row
        else:
            acc[...] += by_row
        for n, k in enumerate(members):
            sec[:, k * size : (k + 1) * size] = by_col[:, n * size : (n + 1) * size]
        if at == len(chunks) - 1:
            for k in range(1, early):
                first_out[k] = finish(acc[k * size : (k + 1) * size], rows_v[k]).astype(BF16)
            if pending[0] is not None:
                queue(None)
            farthest_first(first_copy)
        for k in reversed(members):
            if k:
                second_out[k] = turned(k).astype(BF16)
                queue(second_copy(k))
    total = finish(acc[:size], rows_v[0])
    total_t = turned(0)
    out_ref[...] = total
    queue(None)
    for k in range(1, early):
        first_copy(k).wait_recv()
        total = total + first_in[k].astype(F32)
    for k in reversed(range(1, n_row)):
        second_copy(k).wait_recv()
        total_t = total_t + second_in[k].astype(F32)
    total = total + total_t.T
    for k in late:
        first_copy(k).wait_recv()
        total = total + first_in[k].astype(F32)
    out_ref[...] = total * -inv_v[...]
    for k in range(1, n_col):
        row_copy(k).wait_send()
        first_copy(k).wait_send()
    for k in range(1, n_row):
        col_copy(k).wait_send()
        second_copy(k).wait_send()


def per_device(n_row, n_col, points, abar, inv_scale):
    size, feat = points.shape
    rows = abar.shape[0]
    dma = pltpu.SemaphoreType.DMA
    any_space = pl.BlockSpec(memory_space=pl.ANY)
    total = pl.pallas_call(
        functools.partial(kernel, n_row, n_col),
        out_shape=pltpu.VMEM((size, feat), F32),
        in_specs=[any_space] * 3,
        out_specs=pl.BlockSpec(memory_space=pltpu.VMEM),
        scratch_shapes=[
            pltpu.VMEM((size, feat), BF16),
            pltpu.VMEM((1, feat), F32),
            pltpu.VMEM((rows, n_row, size), BF16),
            pltpu.VMEM((rows * n_row, size), F32),
            pltpu.VMEM((n_col, size, feat), BF16),
            pltpu.VMEM((n_row, size, feat), BF16),
            pltpu.VMEM((n_col, size, feat), BF16),
            pltpu.VMEM((n_row, size, feat), BF16),
            pltpu.VMEM((feat + 16, rows), BF16),
            pltpu.VMEM((n_row, feat, size), BF16),
            pltpu.VMEM((rows, n_row * size), BF16),
            pltpu.VMEM((n_col * size, 2 * feat), F32),
            pltpu.VMEM((feat + 16, n_row * size), F32),
            pltpu.VMEM((n_col, size, feat), BF16),
            pltpu.VMEM((n_row, feat, size), BF16),
            pltpu.VMEM((n_col, size, feat), BF16),
            pltpu.VMEM((n_row, feat, size), BF16),
            dma((3,)),
            dma((n_col,)), dma((n_col,)), dma((n_row,)), dma((n_row,)),
            dma((n_col,)), dma((n_col,)), dma((n_row,)), dma((n_row,)),
        ],
        compiler_params=pltpu.CompilerParams(collective_id=0, has_side_effects=True),
    )(points, inv_scale.reshape(1, feat), abar.reshape(rows, n_row, size))
    return total


def solution(mesh):
    placed = (P(("row", "col"), None), P("row", None, "col", None), P())
    body = functools.partial(per_device, mesh.shape["row"], mesh.shape["col"])
    return jax.shard_map(
        body, mesh=mesh, in_specs=placed, out_specs=P(("row", "col"), None), check_vma=False
    )
```

time: 17.7 us -> 17.2 us (0.972)
  Pallas kernels: 16.9 us -> 16.5 us
    pallas_call x1, Pallas kernels: 16.9 us -> 16.5 us  [per_device(): pl.pallas_call(functools.partial(kernel, n_row, n_col), out_shape=pltpu.V...]
where the time goes in v2:
time: 17.2 us; the launch traced here: 17.1 us
  Pallas kernels  16.5 us (96%)
  local copies, waits for them, and re-layouts  0.63 us (4%)
    pallas_call x1, Pallas kernels, per_device(): pl.pallas_call(functools.partial(kernel, n_row, n_col), out_shape=pltpu.V...  16.5 us
    unnamed x1, local copies, waits for them, and re-layouts  0.63 us

profile of v2, /device:TPU:0, one launch (start us, length us, event | category | flops | bytes accessed | tf_op | source)
XLA Modules:
  0.0 17.1 jit_solution(4488806135836797856)
XLA Ops:
  0.0 16.5 %shard_map.37 = f32[128,128]{1,0:T(8,128)S(1)} custom-call(bf16[128,128]{1,0:T(8,128)(2,1)} %pts_hbm.1, f32[1,128]{1,0:T(1,128)} %bitcast.3, bf16[512,8,128]{2,1,0:T(8,128)(2,1)} %bitcast.2), custom_call_target="tpu_custom_call" | custom-call | tf_op jit(solution)/shard_map/pallas_call | solution.py:266
  16.5 0.6 %copy.5 = f32[128,128]{1,0:T(8,128)} copy(f32[128,128]{1,0:T(8,128)S(1)} %shard_map.37) | data formatting | bytes 131072

commit v3 on v2

--- a/solution.py
+++ b/solution.py
@@ -38,23 +38,20 @@
     return jnp.where((lane >= first) & (lane < first + 3), 1.0, 0.0).astype(BF16)
 
 
-def augment(block, left):
+def augment(block):
     half = half_square(block)
     high = half.astype(BF16).astype(F32)
     mid = (half - high).astype(BF16).astype(F32)
     low = half - high - mid
     lane = lax.broadcasted_iota(jnp.int32, block.shape, 1)
-    shift = 0 if left else 3
-    parts = jnp.where(lane == shift, high, 0.0)
-    parts = jnp.where(lane == shift + 1, mid, parts)
-    parts = jnp.where(lane == shift + 2, low, parts)
-    ones = (lane >= 3 - shift) & (lane < 6 - shift)
-    return jnp.where(ones, 1.0, parts).astype(BF16)
+    parts = jnp.where(lane == 0, high, 0.0)
+    parts = jnp.where(lane == 1, mid, parts)
+    return jnp.where(lane == 2, low, parts).astype(BF16)
 
 
 def kernel(
     n_row, n_col, pts_hbm, inv_hbm, ab_hbm, out_ref,
-    pts_v, inv_v, ab_v, af, rows_v, cols_v, left_aug, right_aug, row_t, col_t,
+    pts_v, inv_v, ab_v, af, rows_v, cols_v, left_aug, col_half, row_t, col_t,
     weighted, acc, sec,
     first_out, second_out, first_in, second_in,
     load_sem, rows_send, rows_recv, cols_send, cols_recv,
@@ -123,14 +120,23 @@
             def _():
                 copy_of(partner(c, c + d, n_col)).start()
 
-    for k in reversed(range(1, n_row)):
+    first_cols = [k for k in reversed(range(1, n_row)) if k >= n_row - 2]
+    for k in first_cols:
         col_copy(k).start()
     farthest_first(row_copy)
-
-    left_aug[0] = augment(own, True)
-    right_aug[0] = augment(own, False)
-    own_t = own.T
-    col_t[0] = own_t
+    for k in reversed(range(1, n_row)):
+        if k not in first_cols:
+            col_copy(k).start()
+
+    left_aug[0] = augment(own)
+
+    def place_col(k, block):
+        turned_block = block.T
+        wide_block = turned_block.astype(F32)
+        col_t[k] = turned_block
+        col_half[k] = -0.5 * jnp.sum(wide_block * wide_block, axis=0, keepdims=True)
+
+    place_col(0, own)
     loads[2].wait()
     step = min(rows, 128)
 
@@ -143,7 +149,6 @@
     lax.fori_loop(0, rows // step, widen, 0)
 
     early = n_col
-    late = list(range(early, n_col))
     wide = n_row * size
     extra = row_t.shape[0] - feat
     groups = [(k, min(k + 2, n_row)) for k in range(0, n_row, 2)]
@@ -156,15 +161,15 @@
     def stack(parts):
         return jnp.concatenate(parts, axis=0) if len(parts) > 1 else parts[0]
 
-    def weigh(some_rows, left, half, groups):
+    def weigh(some_rows, left, groups):
         top, low = some_rows[0] * size, (some_rows[-1] + 1) * size
         for begin, end in groups:
-            right = stack([joined(cols_v[j], right_aug[j]) for j in range(begin, end)])
+            right = stack([joined(cols_v[j], marks(size, feat, 0)) for j in range(begin, end)])
             exponent = lax.dot_general(
                 left, right, (((1,), (1,)), ((), ())), preferred_element_type=F32
             )
-            if half is not None:
-                exponent = exponent + half
+            halves = [col_half[j] for j in range(begin, end)]
+            exponent = exponent + jnp.concatenate(halves, axis=1)
             factors = jnp.concatenate([
                 stack([
                     af[pl.ds(col_from[i] * (size * n_row) + row_from[j], size, stride=n_row), :]
@@ -189,11 +194,11 @@
         return both[:, feat:] * block.astype(F32) - both[:, :feat]
 
     row_t[feat:] = jnp.ones((extra, rows), BF16)
-    row_t[:feat, :size] = own_t
+    row_t[:feat, :size] = own.T
     for k in range(1, early):
         row_copy(k).wait_recv()
     for k in range(1, early):
-        left_aug[k] = augment(rows_v[k], True)
+        left_aug[k] = augment(rows_v[k])
         row_t[:feat, k * size : (k + 1) * size] = rows_v[k].T
     pending = [None]
 
@@ -213,11 +218,10 @@
                 col_copy(k).wait_recv()
         for k in members:
             if k:
-                right_aug[k] = augment(cols_v[k], False)
-                col_t[k] = cols_v[k].T
+                place_col(k, cols_v[k])
         by_row, by_col = weigh(
             list(range(early)),
-            stack([joined(rows_v[i], left_aug[i]) for i in range(early)]), None, chunk,
+            stack([joined(rows_v[i], left_aug[i]) for i in range(early)]), chunk,
         )
         if at == 0:
             acc[...] = by_row
@@ -246,9 +250,6 @@
         second_copy(k).wait_recv()
         total_t = total_t + second_in[k].astype(F32)
     total = total + total_t.T
-    for k in late:
-        first_copy(k).wait_recv()
-        total = total + first_in[k].astype(F32)
     out_ref[...] = total * -inv_v[...]
     for k in range(1, n_col):
         row_copy(k).wait_send()
@@ -276,7 +277,7 @@
             pltpu.VMEM((n_col, size, feat), BF16),
             pltpu.VMEM((n_row, size, feat), BF16),
             pltpu.VMEM((n_col, size, feat), BF16),
-            pltpu.VMEM((n_row, size, feat), BF16),
+            pltpu.VMEM((n_row, 1, size), F32),
             pltpu.VMEM((feat + 16, rows), BF16),
             pltpu.VMEM((n_row, feat, size), BF16),
             pltpu.VMEM((rows, n_row * size), BF16),

time: 17.2 us -> 17.1 us (level)
  Pallas kernels: 16.5 us -> 16.3 us
where the time goes in v3:
time: 17.1 us; the launch traced here: 17 us
  Pallas kernels  16.3 us (95%)
  local copies, waits for them, and re-layouts  0.63 us (4%)
    pallas_call x1, Pallas kernels, per_device(): pl.pallas_call(functools.partial(kernel, n_row, n_col), out_shape=pltpu.V...  16.3 us
    unnamed x1, local copies, waits for them, and re-layouts  0.63 us

profile of v3, /device:TPU:0, one launch (start us, length us, event | category | flops | bytes accessed | tf_op | source)
XLA Modules:
  0.0 17.0 jit_solution(17996004184349366872)
XLA Ops:
  0.0 16.3 %shard_map.37 = f32[128,128]{1,0:T(8,128)S(1)} custom-call(bf16[128,128]{1,0:T(8,128)(2,1)} %pts_hbm.1, f32[1,128]{1,0:T(1,128)} %bitcast.3, bf16[512,8,128]{2,1,0:T(8,128)(2,1)} %bitcast.2), custom_call_target="tpu_custom_call" | custom-call | tf_op jit(solution)/shard_map/pallas_call | solution.py:267
  16.3 0.6 %copy.5 = f32[128,128]{1,0:T(8,128)} copy(f32[128,128]{1,0:T(8,128)S(1)} %shard_map.37) | data formatting | bytes 131072

commit v4 on v3

--- a/solution.py
+++ b/solution.py
@@ -243,13 +243,13 @@
     total_t = turned(0)
     out_ref[...] = total
     queue(None)
-    for k in range(1, early):
-        first_copy(k).wait_recv()
-        total = total + first_in[k].astype(F32)
     for k in reversed(range(1, n_row)):
         second_copy(k).wait_recv()
         total_t = total_t + second_in[k].astype(F32)
     total = total + total_t.T
+    for k in range(1, early):
+        first_copy(k).wait_recv()
+        total = total + first_in[k].astype(F32)
     out_ref[...] = total * -inv_v[...]
     for k in range(1, n_col):
         row_copy(k).wait_send()

time: 17.1 us -> 17 us (level)
  no operation moved by 1% of the time
where the time goes in v4:
time: 17 us; the launch traced here: 16.8 us
  Pallas kernels  16.2 us (95%)
  local copies, waits for them, and re-layouts  0.63 us (4%)
    pallas_call x1, Pallas kernels, per_device(): pl.pallas_call(functools.partial(kernel, n_row, n_col), out_shape=pltpu.V...  16.2 us
    unnamed x1, local copies, waits for them, and re-layouts  0.63 us

profile of v4, /device:TPU:0, one launch (start us, length us, event | category | flops | bytes accessed | tf_op | source)
XLA Modules:
  0.0 16.8 jit_solution(11548647467323195657)
XLA Ops:
  0.0 16.2 %shard_map.37 = f32[128,128]{1,0:T(8,128)S(1)} custom-call(bf16[128,128]{1,0:T(8,128)(2,1)} %pts_hbm.1, f32[1,128]{1,0:T(1,128)} %bitcast.3, bf16[512,8,128]{2,1,0:T(8,128)(2,1)} %bitcast.2), custom_call_target="tpu_custom_call" | custom-call | tf_op jit(solution)/shard_map/pallas_call | solution.py:267
  16.2 0.6 %copy.5 = f32[128,128]{1,0:T(8,128)} copy(f32[128,128]{1,0:T(8,128)S(1)} %shard_map.37) | data formatting | bytes 131072

commit v5 on v4

--- a/solution.py
+++ b/solution.py
@@ -187,8 +187,7 @@
             for begin, end in groups for j in range(begin, end)
         ])
         by_row = jnp.dot(block, every, preferred_element_type=F32)
-        by_col = jnp.dot(row_t[:, top:low], block, preferred_element_type=F32)
-        return by_row, by_col
+        return by_row, lambda: jnp.dot(row_t[:, top:low], block, preferred_element_type=F32)
 
     def finish(both, block):
         return both[:, feat:] * block.astype(F32) - both[:, :feat]
@@ -227,14 +226,15 @@
             acc[...] = by_row
         else:
             acc[...] += by_row
-        for n, k in enumerate(members):
-            sec[:, k * size : (k + 1) * size] = by_col[:, n * size : (n + 1) * size]
         if at == len(chunks) - 1:
             for k in range(1, early):
                 first_out[k] = finish(acc[k * size : (k + 1) * size], rows_v[k]).astype(BF16)
             if pending[0] is not None:
                 queue(None)
             farthest_first(first_copy)
+        by_col = by_col()
+        for n, k in enumerate(members):
+            sec[:, k * size : (k + 1) * size] = by_col[:, n * size : (n + 1) * size]
         for k in reversed(members):
             if k:
                 second_out[k] = turned(k).astype(BF16)

time: 17 us -> 16.9 us (level)
  no operation moved by 1% of the time
where the time goes in v5:
time: 16.9 us; the launch traced here: 16.8 us
  Pallas kernels  16.1 us (95%)
  local copies, waits for them, and re-layouts  0.63 us (4%)
    pallas_call x1, Pallas kernels, per_device(): pl.pallas_call(functools.partial(kernel, n_row, n_col), out_shape=pltpu.V...  16.1 us
    unnamed x1, local copies, waits for them, and re-layouts  0.63 us

profile of v5, /device:TPU:0, one launch (start us, length us, event | category | flops | bytes accessed | tf_op | source)
XLA Modules:
  0.0 16.8 jit_solution(8086145000773086537)
XLA Ops:
  0.0 16.1 %shard_map.37 = f32[128,128]{1,0:T(8,128)S(1)} custom-call(bf16[128,128]{1,0:T(8,128)(2,1)} %pts_hbm.1, f32[1,128]{1,0:T(1,128)} %bitcast.3, bf16[512,8,128]{2,1,0:T(8,128)(2,1)} %bitcast.2), custom_call_target="tpu_custom_call" | custom-call | tf_op jit(solution)/shard_map/pallas_call | solution.py:267
  16.1 0.6 %copy.5 = f32[128,128]{1,0:T(8,128)} copy(f32[128,128]{1,0:T(8,128)S(1)} %shard_map.37) | data formatting | bytes 131072
